TPU v7x, 32 devices: a whole 2x2x4 slice. The times are simulated.
32 devices in a mesh: rep: 4 (over x, core), shard: 8 (over z, y).
Axes of the slice: x: 2, y: 2, z: 4, core: 2. Of those that a mesh axis runs over, the one named last changes fastest.
Arguments:
- dense_out: bfloat16 [4096, 128], P(('rep', 'shard')), may hold values from -0.75 to 0.75
- pooled: bfloat16 [4096, 26, 128], P(('rep', 'shard')), may hold values from -0.75 to 0.75
- top_weight: bfloat16 [479, 1024], replicated, may hold values from -0.25 to 0.25
- top_cotangent: bfloat16 [4096, 1024], P(('rep', 'shard')), may hold values from -3 to 3
- indices: int32 [4096, 26, 2], P(('rep', 'shard')), may hold values from 0 to 2047, as said below
Outputs:
- dense_grad: bfloat16 [4096, 128], P(('rep', 'shard'))
- top_grad: float32 [479, 1024], replicated
- bias_grad: float32 [1024], replicated
- table_grad: float32 [26, 2048, 128], P(None, 'shard')
Inputs may be any that keep to these rules, and one draw needn't show every extreme that they name: `indices`: rows r with r // 256 = s are held by shard s. For every device's 128 samples and every table, at most 16 of the device's lookups fall in any one block of 64 rows starting at a multiple of 64, and some such block holds exactly 16.
All inputs are finite; a program needn't handle non-finite values.
Results may differ from a plain program's by a relative error of at most 0.008.
Values may be sent and summed in bfloat16 or wider, within the bound.
A program may use at most 128 MiB of HBM per device.

v0:
```python
import jax
import jax.numpy as jnp
import numpy as np
from jax import lax
from jax.sharding import PartitionSpec as P

R_SHARD = 256
highest = lax.Precision.HIGHEST


def one_hot_sums(rows, keys, height):
    tables_here = rows.shape[0]
    flat_rows = rows.reshape(tables_here, -1, rows.shape[-1])
    flat_keys = keys.reshape(tables_here, -1)

    def per_table(member):
        table_rows, table_keys = member
        levels = lax.broadcasted_iota(jnp.int32, (height, table_keys.shape[0]), 0)
        matches = (levels == table_keys[None, :]).astype(jnp.bfloat16)
        return jnp.dot(matches, table_rows, preferred_element_type=jnp.float32)

    return lax.map(per_table, (flat_rows, flat_keys))


def pair_table(vectors):
    lower_i, lower_j = np.tril_indices(vectors, -1)
    select = np.zeros((vectors * vectors, lower_i.shape[0]), np.float32)
    select[lower_i * vectors + lower_j, np.arange(lower_i.shape[0])] = 1.0
    mirrored = np.zeros((lower_i.shape[0], vectors * vectors), np.float32)
    mirrored[np.arange(lower_i.shape[0]), lower_i * vectors + lower_j] = 1.0
    mirrored[np.arange(lower_i.shape[0]), lower_j * vectors + lower_i] = 1.0
    return (jnp.asarray(select), jnp.asarray(mirrored))


def on_device(dense_out, pooled, top_weight, top_cotangent, indices):
    samples = dense_out.shape[0]
    emb_width = dense_out.shape[1]
    tables = pooled.shape[1]
    lookups = indices.shape[2]
    replicas = lax.axis_size("rep")
    shards = lax.axis_size("shard")
    vectors = tables + 1
    select, mirrored = pair_table(vectors)
    stacked = jnp.concatenate([dense_out[:, None, :], pooled], axis=1)
    gram_matrix = jnp.einsum("bie,bje->bij", stacked, stacked, preferred_element_type=jnp.float32)
    gram_flat = gram_matrix.reshape(samples, vectors * vectors)
    pair_values = jnp.dot(
        gram_flat, select, precision=highest, preferred_element_type=jnp.float32
    ).astype(jnp.bfloat16)
    joined = jnp.concatenate([dense_out, pair_values], axis=1)
    grad_in = lax.dot_general(
        top_cotangent, top_weight, (((1,), (1,)), ((), ())), preferred_element_type=jnp.float32
    )
    top_part = lax.dot_general(
        joined, top_cotangent, (((0,), (0,)), ((), ())), preferred_element_type=jnp.float32
    )
    bias_part = jnp.sum(top_cotangent, axis=0, dtype=jnp.float32)
    pair_grad = grad_in[:, emb_width:]
    mirror = jnp.dot(
        pair_grad, mirrored, precision=highest, preferred_element_type=jnp.float32
    ).reshape(samples, vectors, vectors)
    mirror_high = mirror.astype(jnp.bfloat16)
    mirror_low = (mirror - mirror_high.astype(jnp.float32)).astype(jnp.bfloat16)
    vec_grad = jnp.einsum("bij,bje->bie", mirror_high, stacked, preferred_element_type=jnp.float32)
    vec_grad = vec_grad + jnp.einsum(
        "bij,bje->bie", mirror_low, stacked, preferred_element_type=jnp.float32
    )
    dense_grad = (grad_in[:, :emb_width] + vec_grad[:, 0]).astype(jnp.bfloat16)
    pooled_grad = vec_grad[:, 1:].astype(jnp.bfloat16)
    row_span = R_SHARD // replicas
    blocks = replicas * shards
    per_block = 2 * samples * lookups // blocks
    count_here = samples * lookups
    capacity = blocks * per_block
    by_table = jnp.transpose(indices, (1, 0, 2)).reshape(tables, count_here)
    lookup_rows = jnp.broadcast_to(
        jnp.transpose(pooled_grad, (1, 0, 2))[:, :, None, :], (tables, samples, lookups, emb_width)
    ).reshape(tables, count_here, emb_width)

    def place_table(member):
        table_keys, table_rows = member
        block_row = table_keys // row_span
        later = lax.broadcasted_iota(jnp.int32, (count_here, count_here), 0)
        sooner = lax.broadcasted_iota(jnp.int32, (count_here, count_here), 1)
        earlier = (block_row[None, :] == block_row[:, None]) & (sooner < later)
        slot_row = block_row * per_block + jnp.sum(earlier, axis=1, dtype=jnp.int32)
        levels = lax.broadcasted_iota(jnp.int32, (capacity, count_here), 0)
        placed = levels == slot_row[None, :]
        rows_out = jnp.dot(
            placed.astype(jnp.bfloat16), table_rows, preferred_element_type=jnp.float32
        ).astype(jnp.bfloat16)
        keys_out = (
            jnp.sum(
                jnp.where(placed, (table_keys % R_SHARD + 1)[None, :], 0), axis=1, dtype=jnp.int32
            )
            - 1
        )
        return (rows_out, keys_out)

    send_rows, send_keys = lax.map(place_table, (by_table, lookup_rows))
    top_grad, bias_grad = lax.psum((top_part, bias_part), ("rep", "shard"))
    grouped_rows = send_rows.reshape(tables, shards, replicas * per_block, emb_width)
    grouped_keys = send_keys.reshape(tables, shards, replicas * per_block)
    partial_value = one_hot_sums(
        lax.all_to_all(grouped_rows, "shard", split_axis=1, concat_axis=1, tiled=True),
        lax.all_to_all(grouped_keys, "shard", split_axis=1, concat_axis=1, tiled=True),
        R_SHARD,
    )
    table_grad = lax.psum(partial_value, "rep")
    return (dense_grad, top_grad, bias_grad, table_grad)


def solution(mesh):
    return jax.shard_map(
        on_device,
        mesh=mesh,
        in_specs=(
            P(("rep", "shard"), None),
            P(("rep", "shard"), None, None),
            P(),
            P(("rep", "shard"), None),
            P(("rep", "shard"), None, None),
        ),
        out_specs=(P(("rep", "shard"), None), P(), P(), P(None, "shard", None)),
        check_vma=False,
    )
```

profile of v0, /device:TPU:0, one launch (start us, length us, event | category | flops | bytes accessed | tf_op | source)
XLA Modules:
  0.0 386.4 jit_solution(17738884548787175198)
XLA Ops:
  9.8 2.0 fusion.17
  17.7 2.8 copy.78
  20.6 2.4 copy.77
  24.8 2.9 copy.79
  27.7 2.2 add.78
  34.0 2.4 broadcast_in_dim.67
  36.3 57.8 %while.25 = (s32[]{:T(128)}, bf16[26,512,128]{2,1,0:T(8,128)(2,1)}, s32[26,512]{1,0:T(8,128)S(1)}, s32[26,256]{1,0:T(8,128)S(1)}, bf16[26,256,128]{2,1,0:T(8,128)(2,1)}, /*index=5*/s32[]{:T(128)}, s32[]{:T(128)}) while((s32[]{:T(128)}, bf16[26,512,128]{2,1,0:T(8,128)(2,1)}, s32[26,512]{1,0:T(8,128)S(1)}, s32[26,256]{1,0:T(8,128)S(1)}, ...), condition=%wide.region_6.7_spmd, body=%wide.region_3.6_spmd.sunk | while | flops 34486784 | bytes 224341 | solution.py:100
  95.0 7.3 %all-to-all-start = ((s32[8,1,1664]{2,1,0:T(1,128)}), s32[8,1,1664]{2,1,0:T(1,128)S(1)}, u32[]{:S(2)}, u32[]{:S(2)}) async-start(s32[8,1,1664]{2,1,0:T(1,128)} %reshape.98), calls=%async_computation | async-start | bytes 106496 | tf_op jit(solution)/shard_map/all_to_all | solution.py:106
  102.3 4.8 %copy.87 = bf16[26,8,64,128]{3,2,0,1:T(8,128)(2,1)} copy(bf16[26,8,64,128]{3,2,1,0:T(8,128)(2,1)} %bitcast.71) | data formatting | bytes 6815744 | tf_op jit(solution)/shard_map/reshape | solution.py:102
  107.1 2.0 all-to-all-done
  109.1 4.5 %all-to-all-start.1 = ((bf16[26,8,64,128]{3,2,0,1:T(8,128)(2,1)}), bf16[26,8,64,128]{3,2,0,1:T(8,128)(2,1)}, u32[]{:S(2)}, u32[]{:S(2)}) async-start(bf16[26,8,64,128]{3,2,0,1:T(8,128)(2,1)} %copy.87), calls=%async_computation.1 | async-start | bytes 6815744 | tf_op jit(solution)/shard_map/all_to_all | solution.py:105
  114.5 2.0 fusion.14
  116.5 2.9 reshape.97
  119.4 2.0 convolution_convert_fusion.1
  124.8 73.4 %all-to-all-done.1 = bf16[26,8,64,128]{3,2,0,1:T(8,128)(2,1)} async-done(((bf16[26,8,64,128]{3,2,0,1:T(8,128)(2,1)}), bf16[26,8,64,128]{3,2,0,1:T(8,128)(2,1)}, u32[]{:S(2)}, u32[]{:S(2)}) %all-to-all-start.1) | async-done | bytes 3407904 | tf_op jit(solution)/shard_map/all_to_all | solution.py:105
  198.2 4.8 %copy.88 = bf16[26,8,64,128]{3,2,1,0:T(8,128)(2,1)} copy(bf16[26,8,64,128]{3,2,0,1:T(8,128)(2,1)} %all-to-all-done.1) | data formatting | bytes 6815744 | tf_op jit(solution)/shard_map/all_to_all | solution.py:105
  203.0 47.0 %while.26 = (s32[]{:T(128)}, f32[26,256,128]{2,1,0:T(8,128)}, s32[26,512]{1,0:T(8,128)S(1)}, bf16[26,512,128]{2,1,0:T(8,128)(2,1)}, s32[]{:T(128)}) while((s32[]{:T(128)}, f32[26,256,128]{2,1,0:T(8,128)}, s32[26,512]{1,0:T(8,128)S(1)}, bf16[26,512,128]{2,1,0:T(8,128)(2,1)}, s32[]{:T(128)}) %tuple.72), condition=%wide.region_8.9_spmd, body=%wide.region_7.8_spmd.sunk | while | flops 33685504 | bytes 269377 | solution.py:22
  219.3 1.8 fusion.47
  226.5 1.8 fusion.47
  237.3 1.8 fusion.47
  251.6 38.0 %psum.22 = f32[1024]{0:T(1024)} all-reduce(f32[1024]{0:T(1024)S(1)} %convert_reduce_fusion.1), channel_id=1, replica_groups=mesh['rep'=4,'shard'=8] {'rep','shard'}, use_global_device_ids=true, to_apply=%region_2.3 | all-reduce | flops 1024 | bytes 8192 | tf_op jit(solution)/shard_map/psum | solution.py:101
  289.6 10.4 %all-reduce.3.cloned.1.call-done = f32[479,1024]{1,0:T(8,128)} async-done(((f32[479,1024]{1,0:T(8,128)}), f32[479,1024]{1,0:T(8,128)}) %all-reduce.3.cloned.1.call-update) | async-done | bytes 1962000 | tf_op jit(solution)/shard_map/psum | solution.py:101
  300.1 74.5 %all-reduce.5.cloned.1.call-done = f32[26,256,128]{2,1,0:T(8,128)} async-done(((f32[26,256,128]{2,1,0:T(8,128)}), f32[26,256,128]{2,1,0:T(8,128)}) %all-reduce.5.cloned.1.call-update) | async-done | bytes 3407888 | tf_op jit(solution)/shard_map/psum | solution.py:109
  374.6 3.2 copy.115
  (334 shorter events, 121.2 us)
Async XLA Ops:
  7.2 1.2 copy-start
  7.2 2.6 copy-start.5
  11.8 4.1 %copy-start.7 = (bf16[128,128]{1,0:T(8,128)(2,1)S(1)}, bf16[128,128]{1,0:T(8,128)(2,1)}, u32[]{:S(2)}) copy-start(bf16[128,128]{1,0:T(8,128)(2,1)} %param.11) | copy-start | bytes 98308
  29.9 1.3 copy-start.1
  31.1 2.6 copy-start.8
  95.0 14.1 %all-to-all-start = ((s32[8,1,1664]{2,1,0:T(1,128)}), s32[8,1,1664]{2,1,0:T(1,128)S(1)}, u32[]{:S(2)}, u32[]{:S(2)}) async-start(s32[8,1,1664]{2,1,0:T(1,128)} %reshape.98), calls=%async_computation | async-start | bytes 106496 | tf_op jit(solution)/shard_map/all_to_all | solution.py:106
  109.1 89.1 %all-to-all-start.1 = ((bf16[26,8,64,128]{3,2,0,1:T(8,128)(2,1)}), bf16[26,8,64,128]{3,2,0,1:T(8,128)(2,1)}, u32[]{:S(2)}, u32[]{:S(2)}) async-start(bf16[26,8,64,128]{3,2,0,1:T(8,128)(2,1)} %copy.87), calls=%async_computation.1 | async-start | bytes 6815744 | tf_op jit(solution)/shard_map/all_to_all | solution.py:105
  113.6 186.5 %all-reduce.3.cloned.1.call-start = ((), (), s32[]{:S(2)}) async-start(), calls=%async_computation.2 | async-start | bytes 3932160 | tf_op jit(solution)/shard_map/psum | solution.py:101
  114.5 4.9 %copy-start.4 = (f32[729,351]{1,0:T(8,128)S(1)}, f32[729,351]{1,0:T(8,128)}, u32[]{:S(2)}) copy-start(f32[729,351]{1,0:T(8,128)} %constant.104.clone) | copy-start | bytes 3070552
  116.5 4.9 %copy-start.3 = (bf16[128,1024]{1,0:T(8,128)(2,1)S(1)}, bf16[128,1024]{1,0:T(8,128)(2,1)}, u32[]{:S(2)}) copy-start(bf16[128,1024]{1,0:T(8,128)(2,1)} %param.14) | copy-start | bytes 786436
  116.5 4.9 %copy-start.6 = (bf16[128,128]{0,1:T(8,128)(2,1)S(1)}, bf16[128,128]{0,1:T(8,128)(2,1)}, u32[]{:S(2)}) copy-start(bf16[128,128]{0,1:T(8,128)(2,1)} %copy.81) | copy-start | bytes 98308
  123.2 251.4 %all-reduce.5.cloned.1.call-start = ((), (), s32[]{:S(2)}) async-start(), calls=%async_computation.3 | async-start | bytes 6815744 | tf_op jit(solution)/shard_map/psum | solution.py:109
  374.6 3.2 copy-start.2
Sparse Core Ops, SparseCore 0:
  123.3 176.7 all-reduce.2
  303.0 71.5 all-reduce.4
where the time goes:
time: 389 us; the launch traced here: 386 us
  waiting for transfers between devices  160 us (41%)
  matrix products  105 us (27%)
  local copies, waits for them, and re-layouts  41.3 us (11%)
  blocking collectives  38 us (10%)
  other arithmetic  14.6 us (4%)
  between operations  14.3 us (4%)
  starting transfers between devices  12 us (3%)
    psum x1, waiting for transfers between devices, on_device(): table_grad = lax.psum(partial_value, 'rep')  74.5 us
    all_to_all x1, waiting for transfers between devices, on_device(): lax.all_to_all(grouped_rows, 'shard', split_axis=1, concat_axis=1, tiled=...  73.4 us
    dot_general x26, matrix products, per_table(): return jnp.dot(matches, table_rows, preferred_element_type=jnp.float32)  46.8 us
    dot_general x26, matrix products, place_table(): jnp.dot(placed.astype(jnp.bfloat16), table_rows, preferred_element_type=j...  45.3 us
    psum x1, blocking collectives, on_device(): top_grad, bias_grad = lax.psum((top_part, bias_part), ('rep', 'shard'))  38 us
    unnamed x25, local copies, waits for them, and re-layouts  11.4 us
    psum x1, waiting for transfers between devices, on_device(): top_grad, bias_grad = lax.psum((top_part, bias_part), ('rep', 'shard'))  10.4 us
  transfers between devices with their start and end apart: 4, of which 4 were waited for; matrix products, arithmetic and copies ran while one was open for 18% of the time, Pallas kernels for 0%

commit v1 on v0

--- a/solution.py
+++ b/solution.py
@@ -106,7 +106,7 @@
         lax.all_to_all(grouped_keys, "shard", split_axis=1, concat_axis=1, tiled=True),
         R_SHARD,
     )
-    table_grad = lax.psum(partial_value, "rep")
+    table_grad = jnp.sum(lax.all_gather(partial_value, "rep"), axis=0)
     return (dense_grad, top_grad, bias_grad, table_grad)
 
 

time: 389 us -> 467 us (1.20)
  waiting for transfers between devices: 160 us -> 230 us
  other arithmetic: 14.6 us -> 22.9 us
    psum x1, waiting for transfers between devices: 10.4 us -> 115 us  [on_device(): top_grad, bias_grad = lax.psum((top_part, bias_part), ('rep', 'shard'))]
    psum x1 -> x0, waiting for transfers between devices: 74.5 us -> none  [on_device(): table_grad = lax.psum(partial_value, 'rep')]
    all_gather x0 -> x1, waiting for transfers between devices: none -> 38.8 us  [on_device(): table_grad = jnp.sum(lax.all_gather(partial_value, 'rep'), axis=0)]
    reduce_sum x0 -> x1, other arithmetic: none -> 8.29 us  [on_device(): table_grad = jnp.sum(lax.all_gather(partial_value, 'rep'), axis=0)]
    unnamed x25 -> x18, local copies, waits for them, and re-layouts: 11.4 us -> 8.33 us
  transfers between devices with their start and end apart: 4 -> 4, of which waited for: 4 -> 4; matrix products, arithmetic and copies ran while one was open for 18% -> 5% of each run, Pallas kernels for 0% -> 0%
where the time goes in v1:
time: 467 us; the launch traced here: 465 us
  waiting for transfers between devices  230 us (49%)
  matrix products  105 us (22%)
  local copies, waits for them, and re-layouts  39.9 us (9%)
  blocking collectives  39.1 us (8%)
  other arithmetic  22.9 us (5%)
  between operations  15.7 us (3%)
  starting transfers between devices  12 us (3%)
    psum x1, waiting for transfers between devices, on_device(): top_grad, bias_grad = lax.psum((top_part, bias_part), ('rep', 'shard'))  115 us
    all_to_all x1, waiting for transfers between devices, on_device(): lax.all_to_all(grouped_rows, 'shard', split_axis=1, concat_axis=1, tiled=...  73.6 us
    dot_general x26, matrix products, per_table(): return jnp.dot(matches, table_rows, preferred_element_type=jnp.float32)  46.8 us
    dot_general x26, matrix products, place_table(): jnp.dot(placed.astype(jnp.bfloat16), table_rows, preferred_element_type=j...  45.3 us
    psum x1, blocking collectives, on_device(): top_grad, bias_grad = lax.psum((top_part, bias_part), ('rep', 'shard'))  39.1 us
    all_gather x1, waiting for transfers between devices, on_device(): table_grad = jnp.sum(lax.all_gather(partial_value, 'rep'), axis=0)  38.8 us
  transfers between devices with their start and end apart: 4, of which 4 were waited for; matrix products, arithmetic and copies ran while one was open for 5% of the time, Pallas kernels for 0%

profile of v1, /device:TPU:0, one launch (start us, length us, event | category | flops | bytes accessed | tf_op | source)
XLA Modules:
  0.0 464.9 jit_solution(4711469768007046253)
XLA Ops:
  11.3 2.0 fusion.17
  17.4 1.8 fusion.15
  19.2 2.9 copy.79
  22.1 2.4 copy.76
  24.5 1.8 fusion.16
  26.3 2.8 copy.78
  29.2 2.2 add.76
  35.2 2.3 broadcast_in_dim.67
  37.5 57.8 %while.25 = (s32[]{:T(128)}, bf16[26,512,128]{2,1,0:T(8,128)(2,1)}, s32[26,512]{1,0:T(8,128)S(1)}, s32[26,256]{1,0:T(8,128)S(1)}, bf16[26,256,128]{2,1,0:T(8,128)(2,1)}, /*index=5*/s32[]{:T(128)}, s32[]{:T(128)}) while((s32[]{:T(128)}, bf16[26,512,128]{2,1,0:T(8,128)(2,1)}, s32[26,512]{1,0:T(8,128)S(1)}, s32[26,256]{1,0:T(8,128)S(1)}, ...), condition=%wide.region_6.7_spmd, body=%wide.region_3.6_spmd.sunk | while | flops 34486784 | bytes 224349 | solution.py:100
  96.2 7.3 %all-to-all-start = ((s32[8,1,1664]{2,1,0:T(1,128)}), s32[8,1,1664]{2,1,0:T(1,128)S(1)}, u32[]{:S(2)}, u32[]{:S(2)}) async-start(s32[8,1,1664]{2,1,0:T(1,128)} %reshape.99), calls=%async_computation | async-start | bytes 106496 | tf_op jit(solution)/shard_map/all_to_all | solution.py:106
  103.5 4.8 %copy.87 = bf16[26,8,64,128]{3,2,0,1:T(8,128)(2,1)} copy(bf16[26,8,64,128]{3,2,1,0:T(8,128)(2,1)} %bitcast.73) | data formatting | bytes 6815744 | tf_op jit(solution)/shard_map/reshape | solution.py:102
  108.3 2.0 all-to-all-done
  110.3 4.5 all-to-all-start.1
  116.6 73.6 %all-to-all-done.1 = bf16[26,8,64,128]{3,2,0,1:T(8,128)(2,1)} async-done(((bf16[26,8,64,128]{3,2,0,1:T(8,128)(2,1)}), bf16[26,8,64,128]{3,2,0,1:T(8,128)(2,1)}, u32[]{:S(2)}, u32[]{:S(2)}) %all-to-all-start.1) | async-done | bytes 3407904 | tf_op jit(solution)/shard_map/all_to_all | solution.py:105
  190.2 4.8 %copy.88 = bf16[26,8,64,128]{3,2,1,0:T(8,128)(2,1)} copy(bf16[26,8,64,128]{3,2,0,1:T(8,128)(2,1)} %all-to-all-done.1) | data formatting | bytes 6815744 | tf_op jit(solution)/shard_map/all_to_all | solution.py:105
  195.0 47.0 %while.26 = (s32[]{:T(128)}, f32[26,256,128]{2,1,0:T(8,128)}, s32[26,512]{1,0:T(8,128)S(1)}, bf16[26,512,128]{2,1,0:T(8,128)(2,1)}, s32[]{:T(128)}) while((s32[]{:T(128)}, f32[26,256,128]{2,1,0:T(8,128)}, s32[26,512]{1,0:T(8,128)S(1)}, bf16[26,512,128]{2,1,0:T(8,128)(2,1)}, s32[]{:T(128)}) %tuple.72), condition=%wide.region_8.9_spmd, body=%wide.region_7.8_spmd.sunk | while | flops 33685504 | bytes 269385 | solution.py:22
  242.8 2.0 fusion.14
  244.8 2.9 reshape.98
  247.7 2.0 convolution_convert_fusion.1
  253.1 39.1 %psum.15 = f32[1024]{0:T(1024)} all-reduce(f32[1024]{0:T(1024)S(1)} %convert_reduce_fusion.1), channel_id=1, replica_groups=mesh['rep'=4,'shard'=8] {'rep','shard'}, use_global_device_ids=true, to_apply=%region_2.3 | all-reduce | flops 1024 | bytes 8192 | tf_op jit(solution)/shard_map/psum | solution.py:101
  292.2 38.8 %all-gather.3.cloned.1.call-done = f32[104,256,128]{2,1,0:T(8,128)} async-done(((f32[26,256,128]{2,1,0:T(8,128)}), f32[104,256,128]{2,1,0:T(8,128)}) %all-gather.3.cloned.1.call-update) | async-done | bytes 13631504 | tf_op jit(solution)/shard_map/all_gather | solution.py:109
  331.0 8.3 %reduce_sum.47 = f32[26,256,128]{2,1,0:T(8,128)} reduce(f32[4,26,256,128]{3,2,1,0:T(8,128)} %bitcast.72, f32[]{:T(128)} %constant.101.clone.1), dimensions={0}, to_apply=%region_9.10 | reduce | flops 2555904 | bytes 17039364 | tf_op jit(solution)/shard_map/reduce_sum | solution.py:109
  339.2 115.2 %all-reduce.2.cloned.1.call-done = f32[479,1024]{1,0:T(8,128)} async-done(((f32[479,1024]{1,0:T(8,128)}), f32[479,1024]{1,0:T(8,128)}) %all-reduce.2.cloned.1.call-update) | async-done | bytes 1962000 | tf_op jit(solution)/shard_map/psum | solution.py:101
  454.4 3.0 copy.114
  (328 shorter events, 121.7 us)
Async XLA Ops:
  8.0 2.0 copy-start
  8.0 3.3 copy-start.4
  31.4 1.2 copy-start.1
  96.2 14.1 %all-to-all-start = ((s32[8,1,1664]{2,1,0:T(1,128)}), s32[8,1,1664]{2,1,0:T(1,128)S(1)}, u32[]{:S(2)}, u32[]{:S(2)}) async-start(s32[8,1,1664]{2,1,0:T(1,128)} %reshape.99), calls=%async_computation | async-start | bytes 106496 | tf_op jit(solution)/shard_map/all_to_all | solution.py:106
  110.3 79.8 %all-to-all-start.1 = ((bf16[26,8,64,128]{3,2,0,1:T(8,128)(2,1)}), bf16[26,8,64,128]{3,2,0,1:T(8,128)(2,1)}, u32[]{:S(2)}, u32[]{:S(2)}) async-start(bf16[26,8,64,128]{3,2,0,1:T(8,128)(2,1)} %copy.87), calls=%async_computation.1 | async-start | bytes 6815744 | tf_op jit(solution)/shard_map/all_to_all | solution.py:105
  114.8 216.2 %all-gather.3.cloned.1.call-start = ((), (), s32[]{:S(2)}) async-start(), calls=%async_computation.3 | async-start | bytes 17039360 | tf_op jit(solution)/shard_map/all_gather | solution.py:109
  241.9 0.8 copy-start.5
  242.0 212.4 %all-reduce.2.cloned.1.call-start = ((), (), s32[]{:S(2)}) async-start(), calls=%async_computation.2 | async-start | bytes 3932160 | tf_op jit(solution)/shard_map/psum | solution.py:101
  242.8 4.8 %copy-start.3 = (f32[729,351]{1,0:T(8,128)S(1)}, f32[729,351]{1,0:T(8,128)}, u32[]{:S(2)}) copy-start(f32[729,351]{1,0:T(8,128)} %constant.104.clone) | copy-start | bytes 3070552
  244.8 4.9 %copy-start.2 = (bf16[128,1024]{1,0:T(8,128)(2,1)S(1)}, bf16[128,1024]{1,0:T(8,128)(2,1)}, u32[]{:S(2)}) copy-start(bf16[128,1024]{1,0:T(8,128)(2,1)} %param.14) | copy-start | bytes 786436
Sparse Core Ops, SparseCore 0:
  242.1 88.8 all-gather.2
Sparse Core Ops, SparseCore 1:
  251.5 202.9 all-reduce.1
